TPU v7x, 512 devices: a 8x2x16 block of a 8x8x16 slice. The times are simulated.
512 devices in a mesh: groups: 2 (over y), expert: 32 (over z, core), tensor: 8 (over x).
Axes of the slice: x: 8, y: 2, z: 16, core: 2. Of those that a mesh axis runs over, the one named last changes fastest.
The devices are a block of a 8x8x16 slice.
Arguments:
- queries: bfloat16 [2048, 4096], P(('groups', 'expert')), parts along dimension 0, may hold values from -200 to 200
- own_kv: bfloat16 [2048, 1024], P(('groups', 'expert')), parts along dimension 0, may hold values from -6 to 6
- prompt_cache: bfloat16 [64, 256, 1024], P(('groups', 'expert'), 'tensor'), parts along dimension 0, may hold values from -8 to 8
- prompt_len: int32 [64], P(('groups', 'expert')), parts along dimension 0, may hold values from 2 to 256
- token_prompt: int32 [2048], P(('groups', 'expert')), parts along dimension 0, may hold values from 0 to 31, as said below
- residual: bfloat16 [2048, 2048], P(('groups', 'expert')), parts along dimension 0, may hold values from -3 to 3
- out_weight: bfloat16 [4096, 2048], P('tensor', 'expert'), may hold values from -0.1875 to 0.1875
- route_ids: int32 [2048, 8], P(('groups', 'expert')), parts along dimension 0, may hold values from 0 to 63, all different within a row; in each aligned block of 32 rows (0 to 31, 32 to 63, ...) at most 6 rows name the same one
- route_weights: float32 [2048, 8], P(('groups', 'expert')), parts along dimension 0, may hold values from 0.05 to 0.3
- w_gate: bfloat16 [64, 2048, 1024], P('expert', None, 'tensor'), may hold values from -0.125 to 0.125
- w_up: bfloat16 [64, 2048, 1024], P('expert', None, 'tensor'), may hold values from -0.125 to 0.125
- w_down: bfloat16 [64, 1024, 2048], P('expert', 'tensor'), may hold values from -0.25 to 0.25
Outputs:
- mixed: bfloat16 [2048, 2048], P(('groups', 'expert'), 'tensor'), parts along dimension 0
There are 2 independent parts, one for each index of `groups`. A program takes and returns all parts, laid end to end along the dimension named above; an argument that names none is the same for every part. Nothing has to cross between parts.
Inputs may be any that keep to these rules, and one draw needn't show every extreme that they name: `token_prompt`: each index of the expert axis holds 2 tokens of each of 16 prompts and none of the others; each prompt has tokens on exactly 16 indices. `route_ids`: A row names distinct experts. Within the 32 rows of one index of the expert axis no expert is named more than 6 times, and in some of these blocks one is named exactly 6 times.
All inputs are finite; a program needn't handle non-finite values.
Results may differ from a plain program's by a relative error of at most 0.015.
Values may be sent and summed in bfloat16 or wider, within the bound.
No kernel may reach another device: no remote copies, remote signals or barrier semaphores. Data moves between devices by JAX's collectives and lax.ppermute only.
A program may use at most 64 MiB of HBM per device.

v0:
```python
import jax
import jax.numpy as jnp
from jax import lax
from jax.sharding import Mesh
from jax.sharding import PartitionSpec as P

HD = 128
EXPERT = ("expert_0", "expert_1")
GROUPS_EXPERT = ("groups", "expert_0", "expert_1")
MASKED_SCORE = -1e30


def combined_all(x, axis, combine):
    everything = jax.tree.map(
        lambda part, kind: lax.all_gather(part.astype(kind), axis),
        x,
        jax.tree.map(lambda a: jnp.bfloat16 if a.dtype == jnp.float32 else a.dtype, x),
    )

    def take(k):
        return jax.tree.map(lambda part, own: part[k].astype(own.dtype), everything, x)

    return lax.fori_loop(
        1, lax.axis_size(axis), lambda k, so_far: combine(so_far, take(k)), take(0)
    )


def sent_to_all(x, axis):
    copies = jnp.broadcast_to(x, (lax.axis_size(axis), *x.shape))
    return lax.all_to_all(copies, axis, split_axis=0, concat_axis=0, tiled=True)


def joined_along(tiles, dim):
    tiles = jnp.moveaxis(tiles, 0, dim)
    shape = tiles.shape
    return tiles.reshape(*shape[:dim], shape[dim] * shape[dim + 1], *shape[dim + 2 :])


def gathered_copies(x, axis, dim):
    tiles = sent_to_all(x, axis)
    return joined_along(tiles, dim)


def in_blocks(x, dim, length):
    shape = x.shape
    tiles = x.reshape(*shape[:dim], length, shape[dim] // length, *shape[dim + 1 :])
    return jnp.moveaxis(tiles, dim, 0)


def exchange_in_order(tiles, axes, sequence):
    shape = [lax.axis_size(a) for a in axes]
    tiles = tiles.reshape(*shape, *tiles.shape[1:])
    for k in sequence:
        tiles = lax.all_to_all(tiles, axes[k], split_axis=k, concat_axis=k, tiled=True)
    return tiles.reshape(-1, *tiles.shape[len(axes) :])


def two_step_exchange(x, groups, sequence, split_dim, concat_dim):
    length = lax.axis_size(groups[0]) * lax.axis_size(groups[1])
    tiles = in_blocks(x, split_dim, length)
    return joined_along(exchange_in_order(tiles, groups, sequence), concat_dim)


def sent_and_summed(x, axis, dim):
    tiles = in_blocks(x, dim, lax.axis_size(axis))
    arrived = lax.all_to_all(tiles, axis, split_axis=0, concat_axis=0, tiled=True)
    return arrived.astype(jnp.float32).sum(axis=0)


def combine_parts(earlier, later):
    top_a, sum_a, value_a = earlier
    top_b, sum_b, value_b = later
    top_score = jnp.maximum(top_a, top_b)
    shrink_a = jnp.exp(top_a - top_score)
    shrink_b = jnp.exp(top_b - top_score)
    return (
        top_score,
        sum_a * shrink_a + sum_b * shrink_b,
        value_a * shrink_a[..., None] + value_b * shrink_b[..., None],
    )


def local(
    queries,
    own_kv,
    prompt_cache,
    prompt_len,
    token_prompt,
    residual,
    out_weight,
    route_ids,
    route_weights,
    w_gate,
    w_up,
    w_down,
):
    tokens = queries.shape[0]
    half_cols = own_kv.shape[1] // 2
    kv_heads = half_cols // HD
    head_count = queries.shape[1] // HD
    group_size = head_count // kv_heads
    score_scale = HD ** (-0.5)
    expert_groups = lax.axis_size(EXPERT)
    fan_count = expert_groups // 2
    per_prompt = tokens // fan_count
    order = jnp.argsort(token_prompt, stable=True)
    inverse = jnp.argsort(order)
    held_prompts = token_prompt[order].reshape(fan_count, per_prompt)[:, 0]
    sorted_query = queries[order].reshape(fan_count, per_prompt, kv_heads, group_size, HD)
    sorted_own = own_kv[order]
    own_keys = sorted_own[:, :half_cols].reshape(fan_count, per_prompt, kv_heads, HD)
    own_values = (
        sorted_own[:, half_cols:].reshape(fan_count, per_prompt, kv_heads, HD).astype(jnp.float32)
    )
    own_score = (
        jnp.einsum("imgjd,imgd->imgj", sorted_query, own_keys, preferred_element_type=jnp.float32)
        * score_scale
    )
    tensor_pos = lax.axis_index("tensor")
    leading = tensor_pos == 0
    start_top = jnp.where(leading, own_score, MASKED_SCORE)
    start_sum = jnp.where(leading, jnp.ones_like(own_score), jnp.zeros_like(own_score))
    start_values = jnp.where(
        leading,
        jnp.broadcast_to(
            own_values[:, :, :, None, :], (fan_count, per_prompt, kv_heads, group_size, HD)
        ),
        0.0,
    )
    block_len = prompt_cache.shape[1]
    positions = tensor_pos * block_len + jnp.arange(block_len, dtype=jnp.int32)
    cache_piece = lax.all_gather(prompt_cache, EXPERT, axis=0, tiled=True)
    length_piece = lax.all_gather(prompt_len, EXPERT, axis=0, tiled=True)
    shard_count = cache_piece.shape[0]
    owners = jnp.arange(shard_count, dtype=jnp.int32)
    matched = owners[:, None] == held_prompts[None, :]
    match_half = matched.astype(jnp.bfloat16)
    match_full = matched.astype(jnp.float32)
    present = jnp.any(matched, 0)
    piece_query = jnp.einsum(
        "qi,imgjd->qmgjd", match_half, sorted_query, preferred_element_type=jnp.float32
    ).astype(jnp.bfloat16)
    key_rows = cache_piece[:, :, :half_cols].reshape(shard_count, block_len, kv_heads, HD)
    value_rows = (
        cache_piece[:, :, half_cols:]
        .reshape(shard_count, block_len, kv_heads, HD)
        .astype(jnp.float32)
    )
    inside = (positions[None, :] < length_piece[:, None])[:, None, None, None, :]
    score_rows = (
        jnp.einsum("qmgjd,qpgd->qmgjp", piece_query, key_rows, preferred_element_type=jnp.float32)
        * score_scale
    )
    score_rows = jnp.where(inside, score_rows, MASKED_SCORE)
    piece_top = jnp.max(score_rows, -1)
    weights = jnp.where(inside, jnp.exp(score_rows - piece_top[..., None]), 0.0)
    piece_sum = jnp.sum(weights, -1)
    piece_values = jnp.einsum("qmgjp,qpgd->qmgjd", weights, value_rows)
    group_top = jnp.einsum("qi,qmgj->imgj", match_full, piece_top)
    group_top = jnp.where(present[:, None, None, None], group_top, MASKED_SCORE)
    group_sum = jnp.einsum("qi,qmgj->imgj", match_full, piece_sum)
    group_values = jnp.einsum("qi,qmgjd->imgjd", match_full, piece_values)
    folded = combine_parts(
        (start_top, start_sum, start_values), (group_top, group_sum, group_values)
    )
    top_score, weight_sum, value_sum = combined_all(folded, "tensor", combine_parts)
    attn_sorted = (value_sum / weight_sum[..., None]).reshape(tokens, head_count * HD)
    attn = attn_sorted[inverse].astype(jnp.bfloat16)
    rows_here = out_weight.shape[0]
    attn_mine = lax.dynamic_slice_in_dim(attn, tensor_pos * rows_here, rows_here, 1)
    column_terms = jnp.dot(
        gathered_copies(attn_mine, EXPERT, 0), out_weight, preferred_element_type=jnp.float32
    )
    partials = two_step_exchange(
        column_terms.astype(jnp.bfloat16), ("expert_0", "expert_1"), (1, 0), 0, 1
    ).astype(column_terms.dtype)
    model_width = residual.shape[1]
    col_width = model_width // lax.axis_size("tensor")
    col_start = tensor_pos * col_width
    resid_cols = lax.dynamic_slice_in_dim(residual, col_start, col_width, 1)
    experts_here = w_gate.shape[0]
    experts = experts_here * expert_groups
    picks = route_ids.shape[1]
    capacity = min(tokens, 3 * tokens * picks // (2 * experts))
    flat_ids = route_ids.reshape(-1)
    expert_marks = (flat_ids[:, None] == jnp.arange(experts, dtype=jnp.int32)[None, :]).astype(
        jnp.int32
    )
    slot_index = jnp.sum((jnp.cumsum(expert_marks, 0) - expert_marks) * expert_marks, 1)
    destination = flat_ids * capacity + slot_index
    source_rows = jnp.arange(tokens * picks, dtype=jnp.int32) // picks
    head_total = sent_and_summed(partials.astype(jnp.bfloat16), "tensor", 1)
    hidden_cols = (resid_cols.astype(jnp.float32) + head_total).astype(jnp.bfloat16)
    outgoing = (
        jnp.zeros((experts * capacity, col_width), jnp.bfloat16)
        .at[destination]
        .set(hidden_cols[source_rows])
    )
    outgoing = outgoing.reshape(expert_groups, experts_here, capacity, col_width)
    arrived = lax.all_to_all(outgoing, EXPERT, split_axis=0, concat_axis=0, tiled=True)
    arrived = gathered_copies(arrived, "tensor", 3)
    gate_proj = jnp.einsum("sxcd,xdf->sxcf", arrived, w_gate, preferred_element_type=jnp.float32)
    up_proj = jnp.einsum("sxcd,xdf->sxcf", arrived, w_up, preferred_element_type=jnp.float32)
    activated = (jax.nn.silu(gate_proj) * up_proj).astype(jnp.bfloat16)
    expert_partials = jnp.einsum(
        "sxcf,xfd->sxcd", activated, w_down, preferred_element_type=jnp.float32
    )
    summed = sent_and_summed(expert_partials.astype(jnp.bfloat16), "tensor", 3).astype(jnp.bfloat16)
    returned = lax.all_to_all(summed, EXPERT, split_axis=0, concat_axis=0, tiled=True).reshape(
        experts * capacity, col_width
    )
    picked = returned[destination].reshape(tokens, picks, col_width).astype(jnp.float32)
    expert_mix = jnp.sum(route_weights[:, :, None] * picked, 1)
    return (hidden_cols.astype(jnp.float32) + expert_mix).astype(jnp.bfloat16)


def solution(mesh):
    split = Mesh(
        mesh.devices.reshape(mesh.shape["groups"], 16, 2, mesh.shape["tensor"]),
        ("groups", "expert_0", "expert_1", "tensor"),
    )
    return jax.shard_map(
        local,
        mesh=split,
        in_specs=(
            P(GROUPS_EXPERT, None),
            P(GROUPS_EXPERT, None),
            P(GROUPS_EXPERT, "tensor", None),
            P(GROUPS_EXPERT),
            P(GROUPS_EXPERT),
            P(GROUPS_EXPERT, None),
            P("tensor", EXPERT),
            P(GROUPS_EXPERT, None),
            P(GROUPS_EXPERT, None),
            P(EXPERT, None, "tensor"),
            P(EXPERT, None, "tensor"),
            P(EXPERT, "tensor", None),
        ),
        out_specs=P(GROUPS_EXPERT, "tensor"),
        check_vma=False,
    )
```

profile of v0, /device:TPU:65, one launch (start us, length us, event | category | flops | bytes accessed | tf_op | source)
XLA Modules:
  0.0 455.3 jit_solution(9609944883478127839)
XLA Ops:
  6.6 0.7 all-gather.6.cloned.1.call-update
  7.4 2.3 sort.34
  9.7 1.6 sort.35
  11.3 1.4 gather_fusion.2
  12.6 0.7 gather_fusion
  14.2 0.6 gather_fusion.1
  15.3 1.3 dynamic-slice
  16.6 0.8 dynamic-update-slice
  17.3 57.1 %all-reduce = s32[32]{0:T(128)S(1)} all-reduce(s32[32]{0:T(128)S(1)} %dynamic-update-slice), channel_id=1, replica_groups=mesh['groups'=2,'expert_0'=16,'expert_1'=2,'tensor'=8] {'expert_0','expe..., use_global_device_ids=true, to_apply=%add | all-reduce | flops 32 | bytes 256
  74.8 1.2 convolution_convert_fusion.1
  76.0 42.0 %all-gather.6.cloned.1.call-done = bf16[32,32,1024]{2,1,0:T(8,128)(2,1)} async-done(((bf16[1,32,1024]{2,1,0:T(8,128)(2,1)}), bf16[32,32,1024]{2,1,0:T(8,128)(2,1)}) %all-gather.6.cloned.1.call-update) | async-done | bytes 2097168 | tf_op jit(solution)/shard_map/all_gather | solution.py:132
  118.1 2.7 fusion.51
  121.1 1.9 fusion.52
  123.2 0.8 fusion.16
  124.3 1.1 reshape.195
  125.4 1.7 convolution_bitcast_fusion
  127.2 1.3 fusion.6
  128.6 20.8 %all-gather = bf16[128,2,4,8]{3,2,1,0:T(4,128)(2,1)S(1)} all-gather(bf16[16,2,4,8]{3,2,1,0:T(4,128)(2,1)S(1)} %copy.80), channel_id=2, replica_groups=mesh['groups'=2,'expert_0'=16,'expert_1'=2,'tensor'=8] {'tensor'}, dimensions={0}, use_global_device_ids=true | all-gather | bytes 18432 | tf_op jit(solution)/shard_map/all_gather | solution.py:15
  149.6 21.1 %all-gather.1 = bf16[128,2,4,8]{3,2,1,0:T(4,128)(2,1)S(1)} all-gather(bf16[16,2,4,8]{3,2,1,0:T(4,128)(2,1)S(1)} %copy.82), channel_id=3, replica_groups=mesh['groups'=2,'expert_0'=16,'expert_1'=2,'tensor'=8] {'tensor'}, dimensions={0}, use_global_device_ids=true | all-gather | bytes 18432 | tf_op jit(solution)/shard_map/all_gather | solution.py:15
  171.3 4.4 all-gather.8.cloned.1.call-done
  175.7 1.0 slice_convert_fusion
  176.8 11.6 %while.19 = (s32[]{:T(128)}, f32[16,2,4,8]{0,3,2,1:T(8,128)S(1)}, f32[16,2,4,8]{0,3,2,1:T(8,128)S(1)}, f32[16,2,4,8,128]{4,3,2,1,0:T(8,128)S(1)}, bf16[8,16,2,4,...) while((s32[]{:T(128)}, f32[16,2,4,8]{0,3,2,1:T(8,128)S(1)}, ...), condition=%wide.region_5.6_spmd, body=%wide.region_4.5_spmd.sunk | while | flops 532485 | bytes 1888407 | solution.py:23
  176.9 1.0 constant_dynamic-slice_fusion.2
  178.1 0.4 fusion.65
  178.6 1.0 constant_dynamic-slice_fusion.2
  179.8 0.4 fusion.65
  180.2 1.0 constant_dynamic-slice_fusion.2
  181.4 0.4 fusion.65
  181.9 1.0 constant_dynamic-slice_fusion.2
  183.1 0.4 fusion.65
  183.5 1.0 constant_dynamic-slice_fusion.2
  184.7 0.4 fusion.65
  185.2 1.0 constant_dynamic-slice_fusion.2
  186.4 0.4 fusion.65
  186.9 1.0 constant_dynamic-slice_fusion.2
  188.1 0.4 fusion.65
  188.9 0.7 gather_fusion.3
  189.7 1.1 broadcast_in_dim.93
  190.8 18.3 %all-to-all-start = ((bf16[32,32,512]{2,1,0:T(8,128)(2,1)}), bf16[32,32,512]{2,1,0:T(8,128)(2,1)S(1)}, u32[]{:S(2)}, u32[]{:S(2)}) async-start(bf16[32,32,512]{2,1,0:T(8,128)(2,1)} %broadcast_in_dim.93), calls=%async_computation | async-start | bytes 2097152 | tf_op jit(solution)/shard_map/all_to_all | solution.py:30
  209.3 0.6 reduce-window.6
  209.9 54.7 %all-to-all-done = bf16[32,32,512]{2,1,0:T(8,128)(2,1)S(1)} async-done(((bf16[32,32,512]{2,1,0:T(8,128)(2,1)}), bf16[32,32,512]{2,1,0:T(8,128)(2,1)S(1)}, u32[]{:S(2)}, u32[]{:S(2)}) %all-to-all-start) | async-done | bytes 1048608 | tf_op jit(solution)/shard_map/all_to_all | solution.py:30
  264.6 0.4 convolution_convert_fusion.2
  265.5 4.0 all_to_all.40
  269.7 0.9 reshape.313
  270.6 4.1 all-to-all-start.2
  275.2 11.5 %all-to-all-done.2 = bf16[16,2,2048]{2,1,0:T(2,128)(2,1)S(1)} async-done(((bf16[16,2,2048]{2,1,0:T(2,128)(2,1)}), bf16[16,2,2048]{2,1,0:T(2,128)(2,1)S(1)}, u32[]{:S(2)}, u32[]{:S(2)}) %all-to-all-start.2) | async-done | bytes 131104 | tf_op jit(solution)/shard_map/all_to_all | solution.py:54
  287.2 0.7 copy.97
  287.9 4.0 all-to-all-start.3
  292.0 7.8 %all-to-all-done.3 = bf16[8,32,256]{2,1,0:T(8,128)(2,1)S(1)} async-done(((bf16[8,32,256]{2,1,0:T(8,128)(2,1)}), bf16[8,32,256]{2,1,0:T(8,128)(2,1)S(1)}, u32[]{:S(2)}, u32[]{:S(2)}) %all-to-all-start.3) | async-done | bytes 131104 | tf_op jit(solution)/shard_map/all_to_all | solution.py:66
  299.9 0.7 add_convert_fusion.1
  300.6 2.2 scatter_custom_fusion
  303.1 27.2 %all_to_all.41 = bf16[32,2,6,256]{3,1,2,0:T(2,128)(2,1)S(1)} all-to-all(bf16[32,2,6,256]{3,1,2,0:T(2,128)(2,1)S(1)} %copy.103), channel_id=1, replica_groups=mesh['groups'=2,'expert_0'=16,'expert_1'=2,'tensor'=8] {'expert_0','expe..., dimensions={0} | all-to-all | bytes 393216 | tf_op jit(solution)/shard_map/all_to_all | solution.py:200
  330.5 40.4 %all_to_all.42 = bf16[8,32,2,6,256]{4,1,3,2,0:T(8,128)(2,1)S(1)} all-to-all(bf16[8,32,2,6,256]{4,1,3,2,0:T(8,128)(2,1)S(1)} %broadcast_in_dim.95), channel_id=1, replica_groups=mesh['groups'=2,'expert_0'=16,'expert_1'=2,'tensor'=8] {'tensor'}, dimensions={0} | all-to-all | bytes 3145728 | tf_op jit(solution)/shard_map/all_to_all | solution.py:30
  371.1 1.0 copy-done.4
  372.1 0.6 convolution_bitcast_fusion.2
  372.7 3.3 convolution_convert_fusion
  376.1 1.6 copy.148
  377.7 40.0 %all_to_all.43 = bf16[8,32,2,6,256]{4,1,3,2,0:T(8,128)(2,1)S(1)} all-to-all(bf16[8,32,2,6,256]{4,1,3,2,0:T(8,128)(2,1)S(1)} %bitcast.142), channel_id=1, replica_groups=mesh['groups'=2,'expert_0'=16,'expert_1'=2,'tensor'=8] {'tensor'}, dimensions={0} | all-to-all | bytes 3145728 | tf_op jit(solution)/shard_map/all_to_all | solution.py:66
  417.7 0.3 reduce_sum.54
  418.0 0.9 copy.108
  418.9 9.0 %all-to-all-start.7 = ((bf16[32,2,6,256]{3,1,2,0:T(2,128)(2,1)}), bf16[32,2,6,256]{3,1,2,0:T(2,128)(2,1)S(1)}, u32[]{:S(2)}, u32[]{:S(2)}) async-start(bf16[32,2,6,256]{3,1,2,0:T(2,128)(2,1)} %copy.108), calls=%async_computation.7 | async-start | bytes 393216 | tf_op jit(solution)/shard_map/all_to_all | solution.py:209
  428.0 18.4 %all-to-all-done.7 = bf16[32,2,6,256]{3,1,2,0:T(2,128)(2,1)S(1)} async-done(((bf16[32,2,6,256]{3,1,2,0:T(2,128)(2,1)}), bf16[32,2,6,256]{3,1,2,0:T(2,128)(2,1)S(1)}, u32[]{:S(2)}, u32[]{:S(2)}) %all-to-all-start.7) | async-done | bytes 196640 | tf_op jit(solution)/shard_map/all_to_all | solution.py:209
  446.5 1.2 gather_fusion.4
  447.8 0.6 add_convert_fusion
  (111 shorter events, 8.0 us)
Async XLA Ops:
  6.5 366.2 %copy-start = (bf16[2,128,2048]{2,1,0:T(8,128)(2,1)S(1)}, bf16[2,128,2048]{2,1,0:T(8,128)(2,1)}, u32[]{:S(2)}) copy-start(bf16[2,128,2048]{2,1,0:T(8,128)(2,1)} %param.25) | copy-start | bytes 3145732
  6.6 6.1 %copy-start.1 = (bf16[32,4096]{1,0:T(8,128)(2,1)S(1)}, bf16[32,4096]{1,0:T(8,128)(2,1)}, u32[]{:S(2)}) copy-start(bf16[32,4096]{1,0:T(8,128)(2,1)} %param.14) | copy-start | bytes 786436
  6.6 111.5 %all-gather.6.cloned.1.call-start = ((), (), s32[]{:S(2)}) async-start(), calls=%async_computation.8 | async-start | bytes 2162688 | tf_op jit(solution)/shard_map/all_gather | solution.py:132
  7.3 168.4 %all-gather.8.cloned.1.call-start = ((), (), s32[]{:S(2)}) async-start(), calls=%async_computation.9 | async-start | bytes 2359296 | tf_op jit(solution)/shard_map/all_gather | solution.py:15
  12.6 1.5 copy-start.2
  122.9 1.4 copy-start.3
  189.7 19.4 %copy-start.6 = (s32[32,8]{0,1:T(8,128)S(1)}, s32[32,8]{0,1:T(8,128)}, u32[]{:S(2)}) copy-start(s32[32,8]{0,1:T(8,128)} %param.21) | copy-start | bytes 3076
  189.7 74.9 %copy-start.5 = (bf16[512,64]{0,1:T(8,128)(2,1)S(1)}, bf16[512,64]{0,1:T(8,128)(2,1)}, u32[]{:S(2)}) copy-start(bf16[512,64]{0,1:T(8,128)(2,1)} %param.20) | copy-start | bytes 196612
  190.8 73.8 %all-to-all-start = ((bf16[32,32,512]{2,1,0:T(8,128)(2,1)}), bf16[32,32,512]{2,1,0:T(8,128)(2,1)S(1)}, u32[]{:S(2)}, u32[]{:S(2)}) async-start(bf16[32,32,512]{2,1,0:T(8,128)(2,1)} %broadcast_in_dim.93), calls=%async_computation | async-start | bytes 2097152 | tf_op jit(solution)/shard_map/all_to_all | solution.py:30
  270.6 16.0 %all-to-all-start.2 = ((bf16[16,2,2048]{2,1,0:T(2,128)(2,1)}), bf16[16,2,2048]{2,1,0:T(2,128)(2,1)S(1)}, u32[]{:S(2)}, u32[]{:S(2)}) async-start(bf16[16,2,2048]{2,1,0:T(2,128)(2,1)} %reshape.313), calls=%async_computation.2 | async-start | bytes 262144 | tf_op jit(solution)/shard_map/all_to_all | solution.py:54
  287.9 12.0 %all-to-all-start.3 = ((bf16[8,32,256]{2,1,0:T(8,128)(2,1)}), bf16[8,32,256]{2,1,0:T(8,128)(2,1)S(1)}, u32[]{:S(2)}, u32[]{:S(2)}) async-start(bf16[8,32,256]{2,1,0:T(8,128)(2,1)} %copy.97), calls=%async_computation.3 | async-start | bytes 262144 | tf_op jit(solution)/shard_map/all_to_all | solution.py:66
  370.9 1.2 copy-start.4
  417.7 10.2 %copy-start.7 = (f32[32,8]{0,1:T(8,128)S(1)}, f32[32,8]{0,1:T(8,128)}, u32[]{:S(2)}) copy-start(f32[32,8]{0,1:T(8,128)} %param.22) | copy-start | bytes 3076
  418.9 27.5 %all-to-all-start.7 = ((bf16[32,2,6,256]{3,1,2,0:T(2,128)(2,1)}), bf16[32,2,6,256]{3,1,2,0:T(2,128)(2,1)S(1)}, u32[]{:S(2)}, u32[]{:S(2)}) async-start(bf16[32,2,6,256]{3,1,2,0:T(2,128)(2,1)} %copy.108), calls=%async_computation.7 | async-start | bytes 393216 | tf_op jit(solution)/shard_map/all_to_all | solution.py:209
Sparse Core Ops, SparseCore 0:
  9.5 108.5 all-gather.5
  128.6 46.9 all-gather.7
where the time goes:
time: 457 us; the launch traced here: 455 us
  blocking collectives  211 us (46%)
  waiting for transfers between devices  140 us (31%)
  starting transfers between devices  35.4 us (8%)
  local copies, waits for them, and re-layouts  31.7 us (7%)
  between operations  14.6 us (3%)
  other arithmetic  11.9 us (3%)
  matrix products  11.1 us (2%)
    unnamed x1, blocking collectives  57.1 us
    all_to_all x1, waiting for transfers between devices, sent_to_all(): return lax.all_to_all(copies, axis, split_axis=0, concat_axis=0, tiled=True)  54.7 us
    all_gather x1, waiting for transfers between devices, local(): cache_piece = lax.all_gather(prompt_cache, EXPERT, axis=0, tiled=True)  42 us
    all_gather x2, blocking collectives, combined_all(): lax.all_gather(part.astype(kind), axis)  41.9 us
    all_to_all x1, blocking collectives, sent_to_all(): return lax.all_to_all(copies, axis, split_axis=0, concat_axis=0, tiled=True)  40.4 us
    all_to_all x1, blocking collectives, sent_and_summed(): lax.all_to_all(tiles, axis, split_axis=0, concat_axis=0, tiled=True)  40 us
    all_to_all x1, blocking collectives, local(): lax.all_to_all(outgoing, EXPERT, split_axis=0, concat_axis=0, tiled=True)  27.2 us
    all_to_all x1, waiting for transfers between devices, local(): lax.all_to_all(summed, EXPERT, split_axis=0, concat_axis=0, tiled=True)  18.4 us
  transfers between devices with their start and end apart: 6, of which 6 were waited for; matrix products, arithmetic and copies ran while one was open for 3% of the time, Pallas kernels for 0%

commit v1 on v0

--- a/solution.py
+++ b/solution.py
@@ -129,7 +129,10 @@
     )
     block_len = prompt_cache.shape[1]
     positions = tensor_pos * block_len + jnp.arange(block_len, dtype=jnp.int32)
-    cache_piece = lax.all_gather(prompt_cache, EXPERT, axis=0, tiled=True)
+    n_dev = lax.axis_size(EXPERT)
+    blocks = jnp.stack([prompt_cache for _ in range(n_dev)])
+    blocks = lax.all_to_all(blocks, EXPERT, split_axis=0, concat_axis=0)
+    cache_piece = jnp.concatenate(blocks, axis=0)
     length_piece = lax.all_gather(prompt_len, EXPERT, axis=0, tiled=True)
     shard_count = cache_piece.shape[0]
     owners = jnp.arange(shard_count, dtype=jnp.int32)

time: 457 us -> 505 us (1.11)
  starting transfers between devices: 35.4 us -> 80.5 us
  waiting for transfers between devices: 140 us -> 105 us
  blocking collectives: 211 us -> 240 us
  local copies, waits for them, and re-layouts: 31.7 us -> 38.2 us
    all_to_all x0 -> x1, starting transfers between devices: none -> 45.5 us  [local(): blocks = lax.all_to_all(blocks, EXPERT, split_axis=0, concat_axis=0)]
    all_gather x1 -> x0, waiting for transfers between devices: 42 us -> none  [local(): cache_piece = lax.all_gather(prompt_cache, EXPERT, axis=0, tiled=True)]
    unnamed x1, blocking collectives: 57.1 us -> 88.6 us
    all_gather x1, waiting for transfers between devices: 4.4 us -> 13 us  [combined_all(): lax.all_gather(part.astype(kind), axis)]
  transfers between devices with their start and end apart: 6 -> 6, of which waited for: 6 -> 5; matrix products, arithmetic and copies ran while one was open for 3% -> 4% of each run, Pallas kernels for 0% -> 0%
where the time goes in v1:
time: 505 us; the launch traced here: 504 us
  blocking collectives  240 us (48%)
  waiting for transfers between devices  105 us (21%)
  starting transfers between devices  80.5 us (16%)
  local copies, waits for them, and re-layouts  38.2 us (8%)
  between operations  14.6 us (3%)
  matrix products  12.5 us (2%)
  other arithmetic  12 us (2%)
    unnamed x1, blocking collectives  88.6 us
    all_to_all x1, waiting for transfers between devices, sent_to_all(): return lax.all_to_all(copies, axis, split_axis=0, concat_axis=0, tiled=True)  54.7 us
    all_to_all x1, starting transfers between devices, local(): blocks = lax.all_to_all(blocks, EXPERT, split_axis=0, concat_axis=0)  45.5 us
    all_to_all x1, blocking collectives, sent_to_all(): return lax.all_to_all(copies, axis, split_axis=0, concat_axis=0, tiled=True)  40.4 us
    all_to_all x1, blocking collectives, sent_and_summed(): lax.all_to_all(tiles, axis, split_axis=0, concat_axis=0, tiled=True)  40 us
    all_gather x2, blocking collectives, combined_all(): lax.all_gather(part.astype(kind), axis)  39.8 us
    all_to_all x1, blocking collectives, local(): lax.all_to_all(outgoing, EXPERT, split_axis=0, concat_axis=0, tiled=True)  27.2 us
    all_to_all x1, waiting for transfers between devices, local(): lax.all_to_all(summed, EXPERT, split_axis=0, concat_axis=0, tiled=True)  18.4 us
  transfers between devices with their start and end apart: 6, of which 5 were waited for; matrix products, arithmetic and copies ran while one was open for 4% of the time, Pallas kernels for 0%

profile of v1, /device:TPU:65, one launch (start us, length us, event | category | flops | bytes accessed | tf_op | source)
XLA Modules:
  0.0 503.8 jit_solution(8630308862392381148)
XLA Ops:
  6.6 2.5 stack.2
  9.1 45.5 %all-to-all-start = ((bf16[32,1,32,1024]{3,2,1,0:T(8,128)(2,1)}), bf16[32,1,32,1024]{3,2,1,0:T(8,128)(2,1)S(1)}, u32[]{:S(2)}, u32[]{:S(2)}) async-start(bf16[32,1,32,1024]{3,2,1,0:T(8,128)(2,1)} %stack.2), calls=%async_computation | async-start | bytes 4194304 | tf_op jit(solution)/shard_map/all_to_all | solution.py:134
  54.7 1.6 sort.34
  56.3 1.6 sort.35
  57.9 0.7 gather_fusion.2
  58.6 1.4 gather_fusion
  60.0 1.0 copy.127
  61.8 0.6 gather_fusion.1
  62.4 0.6 reshape.309
  63.1 1.7 fusion.53
  64.8 0.9 copy.111
  65.7 0.8 convert_select_fusion
  66.5 0.6 select_n.114
  67.2 0.9 copy.83
  68.0 1.3 dynamic-slice
  69.3 0.8 dynamic-update-slice
  70.0 88.6 %all-reduce = s32[32]{0:T(128)S(1)} all-reduce(s32[32]{0:T(128)S(1)} %dynamic-update-slice), channel_id=1, replica_groups=mesh['groups'=2,'expert_0'=16,'expert_1'=2,'tensor'=8] {'expert_0','expe..., use_global_device_ids=true, to_apply=%add | all-reduce | flops 32 | bytes 256
  159.0 1.2 convolution_convert_fusion.1
  160.3 1.7 fusion.51
  161.9 1.3 reshape.201
  163.3 1.9 fusion.52
  165.4 0.8 fusion.16
  166.5 1.1 reshape.202
  167.7 1.7 convolution_bitcast_fusion
  169.4 1.3 fusion.6
  170.8 19.3 %all-gather = bf16[128,2,4,8]{3,2,1,0:T(4,128)(2,1)S(1)} all-gather(bf16[16,2,4,8]{3,2,1,0:T(4,128)(2,1)S(1)} %copy.80), channel_id=2, replica_groups=mesh['groups'=2,'expert_0'=16,'expert_1'=2,'tensor'=8] {'tensor'}, dimensions={0}, use_global_device_ids=true | all-gather | bytes 18432 | tf_op jit(solution)/shard_map/all_gather | solution.py:15
  190.3 20.6 %all-gather.1 = bf16[128,2,4,8]{3,2,1,0:T(4,128)(2,1)S(1)} all-gather(bf16[16,2,4,8]{3,2,1,0:T(4,128)(2,1)S(1)} %copy.82), channel_id=3, replica_groups=mesh['groups'=2,'expert_0'=16,'expert_1'=2,'tensor'=8] {'tensor'}, dimensions={0}, use_global_device_ids=true | all-gather | bytes 18432 | tf_op jit(solution)/shard_map/all_gather | solution.py:15
  211.4 13.0 %all-gather.5.cloned.1.call-done = bf16[128,2,4,8,128]{4,0,3,2,1:T(8,128)(2,1)} async-done(((bf16[16,2,4,8,128]{4,0,3,2,1:T(8,128)(2,1)}), bf16[128,2,4,8,128]{4,0,3,2,1:T(8,128)(2,1)}) %all-gather.5.cloned.1.call-update) | async-done | bytes 2097168 | tf_op jit(solution)/shard_map/all_gather | solution.py:15
  224.4 1.0 slice_convert_fusion
  225.6 11.6 %while.19 = (s32[]{:T(128)}, f32[16,2,4,8]{0,3,2,1:T(8,128)S(1)}, f32[16,2,4,8]{0,3,2,1:T(8,128)S(1)}, f32[16,2,4,8,128]{4,3,2,1,0:T(8,128)S(1)}, bf16[8,16,2,4,...) while((s32[]{:T(128)}, f32[16,2,4,8]{0,3,2,1:T(8,128)S(1)}, ...), condition=%wide.region_5.6_spmd, body=%wide.region_4.5_spmd.sunk | while | flops 532485 | bytes 1888407 | solution.py:23
  225.7 1.0 constant_dynamic-slice_fusion.2
  227.3 1.0 constant_dynamic-slice_fusion.2
  229.0 1.0 constant_dynamic-slice_fusion.2
  230.6 1.0 constant_dynamic-slice_fusion.2
  232.3 1.0 constant_dynamic-slice_fusion.2
  234.0 1.0 constant_dynamic-slice_fusion.2
  235.6 1.0 constant_dynamic-slice_fusion.2
  237.7 0.7 gather_fusion.3
  238.4 1.1 broadcast_in_dim.93
  239.5 18.0 %all-to-all-start.1 = ((bf16[32,32,512]{2,1,0:T(8,128)(2,1)}), bf16[32,32,512]{2,1,0:T(8,128)(2,1)S(1)}, u32[]{:S(2)}, u32[]{:S(2)}) async-start(bf16[32,32,512]{2,1,0:T(8,128)(2,1)} %broadcast_in_dim.93), calls=%async_computation.1 | async-start | bytes 2097152 | tf_op jit(solution)/shard_map/all_to_all | solution.py:30
  257.7 0.6 reduce-window.6
  258.3 54.7 %all-to-all-done.1 = bf16[32,32,512]{2,1,0:T(8,128)(2,1)S(1)} async-done(((bf16[32,32,512]{2,1,0:T(8,128)(2,1)}), bf16[32,32,512]{2,1,0:T(8,128)(2,1)S(1)}, u32[]{:S(2)}, u32[]{:S(2)}) %all-to-all-start.1) | async-done | bytes 1048608 | tf_op jit(solution)/shard_map/all_to_all | solution.py:30
  313.0 0.4 convolution_convert_fusion.2
  313.9 4.2 all_to_all.45
  318.3 0.9 reshape.320
  319.2 4.0 all-to-all-start.3
  323.6 11.5 %all-to-all-done.3 = bf16[16,2,2048]{2,1,0:T(2,128)(2,1)S(1)} async-done(((bf16[16,2,2048]{2,1,0:T(2,128)(2,1)}), bf16[16,2,2048]{2,1,0:T(2,128)(2,1)S(1)}, u32[]{:S(2)}, u32[]{:S(2)}) %all-to-all-start.3) | async-done | bytes 131104 | tf_op jit(solution)/shard_map/all_to_all | solution.py:54
  335.6 0.7 copy.97
  336.3 4.0 all-to-all-start.4
  340.5 7.8 %all-to-all-done.4 = bf16[8,32,256]{2,1,0:T(8,128)(2,1)S(1)} async-done(((bf16[8,32,256]{2,1,0:T(8,128)(2,1)}), bf16[8,32,256]{2,1,0:T(8,128)(2,1)S(1)}, u32[]{:S(2)}, u32[]{:S(2)}) %all-to-all-start.4) | async-done | bytes 131104 | tf_op jit(solution)/shard_map/all_to_all | solution.py:66
  348.4 0.7 add_convert_fusion.1
  349.1 2.2 scatter_custom_fusion
  351.6 27.2 %all_to_all.46 = bf16[32,2,6,256]{3,1,2,0:T(2,128)(2,1)S(1)} all-to-all(bf16[32,2,6,256]{3,1,2,0:T(2,128)(2,1)S(1)} %copy.103), channel_id=1, replica_groups=mesh['groups'=2,'expert_0'=16,'expert_1'=2,'tensor'=8] {'expert_0','expe..., dimensions={0} | all-to-all | bytes 393216 | tf_op jit(solution)/shard_map/all_to_all | solution.py:203
  379.0 40.4 %all_to_all.47 = bf16[8,32,2,6,256]{4,1,3,2,0:T(8,128)(2,1)S(1)} all-to-all(bf16[8,32,2,6,256]{4,1,3,2,0:T(8,128)(2,1)S(1)} %broadcast_in_dim.95), channel_id=1, replica_groups=mesh['groups'=2,'expert_0'=16,'expert_1'=2,'tensor'=8] {'tensor'}, dimensions={0} | all-to-all | bytes 3145728 | tf_op jit(solution)/shard_map/all_to_all | solution.py:30
  419.6 1.0 copy-done.5
  420.6 0.6 convolution_bitcast_fusion.2
  421.2 3.4 convolution_convert_fusion
  424.6 1.6 copy.148
  426.2 40.0 %all_to_all.48 = bf16[8,32,2,6,256]{4,1,3,2,0:T(8,128)(2,1)S(1)} all-to-all(bf16[8,32,2,6,256]{4,1,3,2,0:T(8,128)(2,1)S(1)} %bitcast.145), channel_id=1, replica_groups=mesh['groups'=2,'expert_0'=16,'expert_1'=2,'tensor'=8] {'tensor'}, dimensions={0} | all-to-all | bytes 3145728 | tf_op jit(solution)/shard_map/all_to_all | solution.py:66
  466.5 0.9 copy.108
  467.4 9.0 %all-to-all-start.8 = ((bf16[32,2,6,256]{3,1,2,0:T(2,128)(2,1)}), bf16[32,2,6,256]{3,1,2,0:T(2,128)(2,1)S(1)}, u32[]{:S(2)}, u32[]{:S(2)}) async-start(bf16[32,2,6,256]{3,1,2,0:T(2,128)(2,1)} %copy.108), calls=%async_computation.8 | async-start | bytes 393216 | tf_op jit(solution)/shard_map/all_to_all | solution.py:212
  476.5 18.4 %all-to-all-done.8 = bf16[32,2,6,256]{3,1,2,0:T(2,128)(2,1)S(1)} async-done(((bf16[32,2,6,256]{3,1,2,0:T(2,128)(2,1)}), bf16[32,2,6,256]{3,1,2,0:T(2,128)(2,1)S(1)}, u32[]{:S(2)}, u32[]{:S(2)}) %all-to-all-start.8) | async-done | bytes 196640 | tf_op jit(solution)/shard_map/all_to_all | solution.py:212
  495.0 1.2 gather_fusion.4
  496.3 0.6 add_convert_fusion
  (115 shorter events, 10.3 us)
Async XLA Ops:
  6.5 414.7 %copy-start = (bf16[2,128,2048]{2,1,0:T(8,128)(2,1)S(1)}, bf16[2,128,2048]{2,1,0:T(8,128)(2,1)}, u32[]{:S(2)}) copy-start(bf16[2,128,2048]{2,1,0:T(8,128)(2,1)} %param.25) | copy-start | bytes 3145732
  9.1 45.6 %copy-start.1 = (s32[32]{0:T(128)S(1)}, s32[32]{0:T(128)}, u32[]{:S(2)}) copy-start(s32[32]{0:T(128)} %param.18) | copy-start | bytes 388
  9.1 49.5 %copy-start.2 = (bf16[32,4096]{1,0:T(8,128)(2,1)S(1)}, bf16[32,4096]{1,0:T(8,128)(2,1)}, u32[]{:S(2)}) copy-start(bf16[32,4096]{1,0:T(8,128)(2,1)} %param.14) | copy-start | bytes 786436
  9.1 151.2 %all-to-all-start = ((bf16[32,1,32,1024]{3,2,1,0:T(8,128)(2,1)}), bf16[32,1,32,1024]{3,2,1,0:T(8,128)(2,1)S(1)}, u32[]{:S(2)}, u32[]{:S(2)}) async-start(bf16[32,1,32,1024]{3,2,1,0:T(8,128)(2,1)} %stack.2), calls=%async_computation | async-start | bytes 4194304 | tf_op jit(solution)/shard_map/all_to_all | solution.py:134
  54.6 169.9 %all-gather.5.cloned.1.call-start = ((), (), s32[]{:S(2)}) async-start(), calls=%async_computation.9 | async-start | bytes 2359296 | tf_op jit(solution)/shard_map/all_gather | solution.py:15
  58.6 3.2 copy-start.3
  62.4 3.3 copy-start.6
  165.1 1.4 copy-start.4
  238.4 19.1 %copy-start.8 = (s32[32,8]{0,1:T(8,128)S(1)}, s32[32,8]{0,1:T(8,128)}, u32[]{:S(2)}) copy-start(s32[32,8]{0,1:T(8,128)} %param.21) | copy-start | bytes 3076
  238.4 74.6 %copy-start.7 = (bf16[512,64]{0,1:T(8,128)(2,1)S(1)}, bf16[512,64]{0,1:T(8,128)(2,1)}, u32[]{:S(2)}) copy-start(bf16[512,64]{0,1:T(8,128)(2,1)} %param.20) | copy-start | bytes 196612
  239.5 73.5 %all-to-all-start.1 = ((bf16[32,32,512]{2,1,0:T(8,128)(2,1)}), bf16[32,32,512]{2,1,0:T(8,128)(2,1)S(1)}, u32[]{:S(2)}, u32[]{:S(2)}) async-start(bf16[32,32,512]{2,1,0:T(8,128)(2,1)} %broadcast_in_dim.93), calls=%async_computation.1 | async-start | bytes 2097152 | tf_op jit(solution)/shard_map/all_to_all | solution.py:30
  319.2 15.9 %all-to-all-start.3 = ((bf16[16,2,2048]{2,1,0:T(2,128)(2,1)}), bf16[16,2,2048]{2,1,0:T(2,128)(2,1)S(1)}, u32[]{:S(2)}, u32[]{:S(2)}) async-start(bf16[16,2,2048]{2,1,0:T(2,128)(2,1)} %reshape.320), calls=%async_computation.3 | async-start | bytes 262144 | tf_op jit(solution)/shard_map/all_to_all | solution.py:54
  336.3 12.1 %all-to-all-start.4 = ((bf16[8,32,256]{2,1,0:T(8,128)(2,1)}), bf16[8,32,256]{2,1,0:T(8,128)(2,1)S(1)}, u32[]{:S(2)}, u32[]{:S(2)}) async-start(bf16[8,32,256]{2,1,0:T(8,128)(2,1)} %copy.97), calls=%async_computation.4 | async-start | bytes 262144 | tf_op jit(solution)/shard_map/all_to_all | solution.py:66
  419.4 1.2 copy-start.5
  466.2 10.2 %copy-start.9 = (f32[32,8]{0,1:T(8,128)S(1)}, f32[32,8]{0,1:T(8,128)}, u32[]{:S(2)}) copy-start(f32[32,8]{0,1:T(8,128)} %param.22) | copy-start | bytes 3076
  467.4 27.5 %all-to-all-start.8 = ((bf16[32,2,6,256]{3,1,2,0:T(2,128)(2,1)}), bf16[32,2,6,256]{3,1,2,0:T(2,128)(2,1)S(1)}, u32[]{:S(2)}, u32[]{:S(2)}) async-start(bf16[32,2,6,256]{3,1,2,0:T(2,128)(2,1)} %copy.108), calls=%async_computation.8 | async-start | bytes 393216 | tf_op jit(solution)/shard_map/all_to_all | solution.py:212
Sparse Core Ops, SparseCore 0:
  170.8 53.5 all-gather.4
